TPU v7x, 32 devices: a whole 2x2x4 slice. The times are simulated.
32 devices in a mesh: lat: 16 (over z, y, x), dp: 2 (over core).
Axes of the slice: x: 2, y: 2, z: 4, core: 2. Of those that a mesh axis runs over, the one named last changes fastest.
Arguments:
- state: float32 [2, 128, 256, 128], P('dp', 'lat'), may hold values from -6 to 6
- cotangent: float32 [2, 128, 256, 128], P('dp', 'lat'), may hold values from -0.18 to 0.18
- w_first: bfloat16 [128, 1024], replicated, may hold values from -0.5 to 0.5
- w_middle: bfloat16 [1024, 1024], replicated, may hold values from -0.1875 to 0.1875
- w_last: bfloat16 [1024, 128], replicated, may hold values from -0.1875 to 0.1875
Outputs:
- final_state: float32 [2, 128, 256, 128], P('dp', 'lat')
- grad_first: float32 [128, 1024], replicated
- grad_middle: float32 [1024, 1024], replicated
- grad_last: float32 [1024, 128], replicated
All inputs are finite; a program needn't handle non-finite values.
Results may differ from a plain program's by a relative error of at most 0.0048.
Values sent between devices are 32-bit elements; how exact they have to be, the bound alone decides.
A program may use at most 128 MiB of HBM per device.

v0:
```python
import math

import jax
import jax.numpy as jnp
from jax import lax
from jax.sharding import PartitionSpec as P

MW = 64
STEPS = 2


highest = lax.Precision.HIGHEST
tend_weight = 0.5


def grid_tables(lon_count, wave_count):
    lon_index = jnp.arange(lon_count, dtype=jnp.int32)
    wave_index = jnp.arange(wave_count, dtype=jnp.int32)
    phase_angle = (lon_index[:, None] * wave_index[None, :] % lon_count).astype(jnp.float32) * (
        2.0 * math.pi / lon_count
    )
    cosine = jnp.cos(phase_angle)
    sine_part = jnp.sin(phase_angle)
    analysis = jnp.stack([cosine, -sine_part], axis=2) / lon_count
    factor = jnp.where(wave_index == 0, 1.0, 2.0).astype(jnp.float32)
    synthesis = jnp.stack([cosine, -sine_part], axis=2) * factor[None, :, None]
    return (analysis, synthesis)


def legendre(wave_ids, lat_count, wave_count):
    lat_index = jnp.arange(lat_count).astype(jnp.float32)
    latitude = (lat_index + 0.5) * (math.pi / lat_count) - 0.5 * math.pi
    sine_lat = jnp.sin(latitude)
    cosine_lat = jnp.cos(latitude)
    quad_weight = cosine_lat * (math.pi / lat_count)
    order_m = wave_ids.astype(jnp.float32)
    counter = jnp.arange(1, wave_count).astype(jnp.float32)
    increments = 0.5 * jnp.log((2.0 * counter + 1.0) / (2.0 * counter))
    summed = jnp.sum(
        jnp.where(counter[None, :] <= order_m[:, None], increments[None, :], 0.0), axis=1
    )
    diagonal = jnp.exp(
        0.5 * math.log(0.5) + summed[:, None] + order_m[:, None] * jnp.log(cosine_lat)[None, :]
    )

    def advance(carry, offset):
        previous, current, ratio_prev = carry
        degree = order_m + offset
        ratio_new = jnp.sqrt((4.0 * degree * degree - 1.0) / (degree * degree - order_m * order_m))
        following = ratio_new[:, None] * (
            sine_lat[None, :] * current - previous / ratio_prev[:, None]
        )
        return ((current, following, ratio_new), following)

    initial = (jnp.zeros_like(diagonal), diagonal, jnp.ones_like(order_m))
    _, remaining = lax.scan(advance, initial, jnp.arange(1, wave_count).astype(jnp.float32))
    poly_table = jnp.concatenate([diagonal[None], remaining], axis=0).transpose(1, 0, 2)
    degree = order_m[:, None] + jnp.arange(wave_count).astype(jnp.float32)[None, :]
    kept_mask = degree <= wave_count - 1
    poly_table = jnp.where(kept_mask[:, :, None], poly_table, 0.0)
    damping = jnp.where(
        kept_mask, 1.0 / (1.0 + degree * (degree + 1.0) / (wave_count * (wave_count - 1.0))), 0.0
    )
    return (poly_table, quad_weight, damping)


def silu_slope(value):
    gate_sig = jax.nn.sigmoid(value)
    return gate_sig * (1.0 + value * (1.0 - gate_sig))


def hidden_rows(rows, w_first, w_middle):
    pre_first = jnp.dot(rows, w_first, preferred_element_type=jnp.float32)
    hidden_first = jax.nn.silu(pre_first).astype(jnp.bfloat16)
    pre_middle = jnp.dot(hidden_first, w_middle, preferred_element_type=jnp.float32)
    hidden_middle = jax.nn.silu(pre_middle).astype(jnp.bfloat16)
    return (pre_first, hidden_first, pre_middle, hidden_middle)


def body(state, cotangent, w_first, w_middle, w_last):
    sample, lat_rows, lon_count, features = state.shape
    hidden_count = w_first.shape[1]
    band_count = lax.axis_size("lat")
    lat_count = lat_rows * band_count
    local_waves = MW // band_count
    wave_ids = lax.axis_index("lat") * local_waves + jnp.arange(local_waves, dtype=jnp.int32)
    analysis, synthesis = grid_tables(lon_count, MW)
    poly_table, quad_weight, damping = legendre(wave_ids, lat_count, MW)
    weighted = poly_table * quad_weight[None, None, :]
    row_count = sample * lat_rows * lon_count

    def spectral(field, first, last, in_table, out_table):
        wave_grid = jnp.einsum("bjxf,xmp->bjmpf", field, first, precision=highest)
        coeffs = (
            jnp.einsum(
                "mkj,bjmpf->bmkpf",
                in_table,
                lax.all_to_all(wave_grid, "lat", split_axis=2, concat_axis=1, tiled=True),
                precision=highest,
            )
            * damping[None, :, :, None, None]
        )
        back_grid = jnp.einsum("mkj,bmkpf->bjmpf", out_table, coeffs, precision=highest)
        back_bands = lax.all_to_all(back_grid, "lat", split_axis=1, concat_axis=2, tiled=True)
        return jnp.einsum("bjmpf,xmp->bjxf", back_bands, last, precision=highest)

    saved = []
    field = state
    for step_index in range(STEPS):
        rows = field.reshape(row_count, features).astype(jnp.bfloat16)
        pre_first, hidden_first, pre_middle, hidden_middle = hidden_rows(rows, w_first, w_middle)
        tendency = jnp.dot(hidden_middle, w_last, preferred_element_type=jnp.float32)
        saved.append((rows, pre_first, hidden_first, pre_middle, hidden_middle))
        moved = field + tend_weight * tendency.reshape(field.shape)
        field = spectral(moved, analysis, synthesis, weighted, poly_table)
    grad = cotangent
    total_first = jnp.zeros((features, hidden_count), jnp.float32)
    total_middle = jnp.zeros((hidden_count, hidden_count), jnp.float32)
    total_last = jnp.zeros((hidden_count, features), jnp.float32)
    for step_index in reversed(range(STEPS)):
        pulled = spectral(grad, synthesis, analysis, poly_table, weighted)
        scaled = (tend_weight * pulled).astype(jnp.bfloat16).reshape(row_count, features)
        rows, pre_first, hidden_first, pre_middle, hidden_middle = saved[step_index]
        total_last = total_last + jnp.dot(
            hidden_middle.T, scaled, preferred_element_type=jnp.float32
        )
        middle_back = jnp.dot(scaled, w_last.T, preferred_element_type=jnp.float32)
        middle_grad = (middle_back * silu_slope(pre_middle)).astype(jnp.bfloat16)
        total_middle = total_middle + jnp.dot(
            hidden_first.T, middle_grad, preferred_element_type=jnp.float32
        )
        first_back = jnp.dot(middle_grad, w_middle.T, preferred_element_type=jnp.float32)
        first_grad = (first_back * silu_slope(pre_first)).astype(jnp.bfloat16)
        total_first = total_first + jnp.dot(rows.T, first_grad, preferred_element_type=jnp.float32)
        if step_index > 0:
            back_rows = jnp.dot(first_grad, w_first.T, preferred_element_type=jnp.float32)
            grad = pulled + back_rows.reshape(field.shape)
    total_first, total_middle, total_last = lax.psum(
        (total_first, total_middle, total_last), ("lat", "dp")
    )
    return (field, total_first, total_middle, total_last)


def solution(mesh):
    in_specs = (P("dp", "lat", None, None), P("dp", "lat", None, None), P(), P(), P())
    out_specs = (P("dp", "lat", None, None), P(), P(), P())
    return jax.shard_map(body, mesh=mesh, in_specs=in_specs, out_specs=out_specs, check_vma=False)
```

profile of v0, /device:TPU:0, one launch (start us, length us, event | category | flops | bytes accessed | tf_op | source)
XLA Modules:
  0.0 529.4 jit_solution(4078306409934869593)
XLA Ops:
  7.5 2.1 convolution_bitcast_fusion.7
  10.7 8.3 %all-to-all-start.4 = ((f32[1,8,64,2,128]{4,1,3,0,2:T(8,128)}), f32[1,8,64,2,128]{4,1,3,0,2:T(8,128)S(1)}, u32[]{:S(2)}, u32[]{:S(2)}) async-start(f32[1,8,64,2,128]{4,1,3,0,2:T(8,128)} %copy.120), calls=%async_computation.4 | async-start | bytes 1048576 | tf_op jit(solution)/shard_map/all_to_all | solution.py:98
  19.4 132.3 %while.21 = (s32[]{:T(128)}, f32[4,128]{1,0:T(4,128)S(1)}, f32[4,128]{1,0:T(4,128)S(1)}, f32[4]{0:T(128)S(1)}, f32[63,4,128]{2,0,1:T(8,128)S(1)}, /*index=5*/f32[63]{0:T(128)S(1)}, s32[]{:T(128)}, s32[]{:T(128)}, s32[]{:T(128)}) while((s32[]{:T(128)}, f32[4,128]{1,0:T(4,128)S(1)}, f32[4,128]{1,0:T(4,128)S(1)}, ...), condition=%wide.region_2.3_spmd.clone.clone.clone, body=%wide.region_1.2_spmd.clone.clone.clone.sunk | while | flops 2655 | bytes 19695 | solution.py:56
  151.7 1.3 convert_element_type.118
  153.9 2.2 fusion.108
  156.1 7.9 %multiply_convert_fusion.6 = (bf16[2048,1024]{1,0:T(8,128)(2,1)S(1)}, f32[2048,1024]{1,0:T(8,128)}) fusion(bf16[1024,1024]{1,0:T(8,128)(2,1)S(1)} %copy-done, f32[2048,1024]{1,0:T(8,128)S(1)} %fusion.108), kind=kOutput, calls=%fused_computation.27 | convolution fusion | flops 4315938816 | bytes 23068672 | tf_op jit(solution)/shard_map/dot_general | solution.py:75
  164.0 2.0 copy-done.1
  166.0 1.3 convolution_multiply_fusion.1
  168.0 1.1 copy.109
  169.2 6.9 %all-to-all-start = ((f32[1,8,64,2,128]{4,1,3,0,2:T(8,128)}), f32[1,8,64,2,128]{4,1,3,0,2:T(8,128)S(1)}, u32[]{:S(2)}, u32[]{:S(2)}) async-start(f32[1,8,64,2,128]{4,1,3,0,2:T(8,128)} %copy.109), calls=%async_computation | async-start | bytes 1048576 | tf_op jit(solution)/shard_map/all_to_all | solution.py:98
  178.9 11.7 %all-to-all-done = f32[1,8,64,2,128]{4,1,3,0,2:T(8,128)S(1)} async-done(((f32[1,8,64,2,128]{4,1,3,0,2:T(8,128)}), f32[1,8,64,2,128]{4,1,3,0,2:T(8,128)S(1)}, u32[]{:S(2)}, u32[]{:S(2)}) %all-to-all-start) | async-done | bytes 524320 | tf_op jit(solution)/shard_map/all_to_all | solution.py:98
  190.6 3.9 all-to-all-start.5
  197.1 11.9 %all-to-all-done.5 = f32[1,128,4,2,128]{4,3,2,0,1:T(2,128)S(1)} async-done(((f32[1,128,4,2,128]{4,3,2,0,1:T(2,128)}), f32[1,128,4,2,128]{4,3,2,0,1:T(2,128)S(1)}, u32[]{:S(2)}, u32[]{:S(2)}) %all-to-all-start.5) | async-done | bytes 524320 | tf_op jit(solution)/shard_map/all_to_all | solution.py:104
  209.0 4.5 all-to-all-start.1
  214.0 1.9 multiply_convert_fusion.8
  215.8 11.8 %all-to-all-done.1 = f32[1,128,4,2,128]{4,3,2,0,1:T(2,128)} async-done(((f32[1,128,4,2,128]{4,3,2,0,1:T(2,128)}), f32[1,128,4,2,128]{4,3,2,0,1:T(2,128)}, u32[]{:S(2)}, u32[]{:S(2)}) %all-to-all-start.1) | async-done | bytes 524320 | tf_op jit(solution)/shard_map/all_to_all | solution.py:104
  227.6 1.1 copy.166
  229.1 2.1 fusion.107
  231.2 3.6 multiply_convert_fusion.5
  234.8 6.8 %multiply_convert_fusion.4 = (bf16[2048,1024]{1,0:T(8,128)(2,1)}, f32[2048,1024]{1,0:T(8,128)S(1)}) fusion(bf16[2048,1024]{1,0:T(8,128)(2,1)S(1)} %get-tuple-element.221, bf16[1024,1024]{1,0:T(8,128)(2,1)S(1)} %copy-done), kind=kOutput, calls=%fused_computation.23 | convolution fusion | flops 4305453056 | bytes 18874368 | tf_op jit(solution)/shard_map/dot_general | solution.py:75
  241.7 3.6 multiply_convert_fusion.3
  245.3 17.1 %multiply_convert_fusion.2 = bf16[2048,1024]{1,0:T(8,128)(2,1)S(1)} fusion(f32[2048,1024]{1,0:T(8,128)S(1)} %get-tuple-element.222, bf16[2048,1024]{1,0:T(8,128)(2,1)S(1)} %multiply_convert_fusion.3, bf16[1024,1024]{1,0:T(8,128)(2,1)S(1)} %copy-done), kind=kOutput, calls=%fused_computation.21 | convolution fusion | flops 4313841664 | bytes 18874368 | tf_op jit(solution)/shard_map/dot_general | solution.py:132
  262.4 2.0 copy-done.3
  264.4 1.3 fusion.109
  266.5 1.1 copy.125
  267.6 4.3 all-to-all-start.6
  271.9 4.4 fusion.111
  276.2 3.5 convolution_multiply_fusion
  279.7 6.0 %all-to-all-done.6 = f32[1,8,64,2,128]{4,1,3,0,2:T(8,128)} async-done(((f32[1,8,64,2,128]{4,1,3,0,2:T(8,128)}), f32[1,8,64,2,128]{4,1,3,0,2:T(8,128)}, u32[]{:S(2)}, u32[]{:S(2)}) %all-to-all-start.6) | async-done | bytes 524320 | tf_op jit(solution)/shard_map/all_to_all | solution.py:98
  285.7 1.5 fusion.26
  287.2 1.9 convolution_bitcast_fusion.4
  289.1 2.0 copy.127
  291.1 4.2 all-to-all-start.7
  295.4 10.1 %fusion.110 = f32[1024,1024]{1,0:T(8,128)} fusion(bf16[2048,1024]{1,0:T(8,128)(2,1)} %copy-done.17, bf16[2048,1024]{1,0:T(8,128)(2,1)} %copy-done.18), kind=kOutput, calls=%fused_computation.157 | convolution fusion | flops 4294967296 | bytes 12582912 | tf_op jit(solution)/shard_map/dot_general | solution.py:129
  305.5 3.4 all-to-all-done.7
  308.9 1.1 copy.163
  311.5 7.2 %multiply_convert_fusion.1 = bf16[2048,1024]{1,0:T(8,128)(2,1)} fusion(f32[2048,1024]{1,0:T(8,128)} %get-tuple-element.218, bf16[2048,128]{1,0:T(8,128)(2,1)S(1)} %bitcast.312, bf16[1024,128]{1,0:T(8,128)(2,1)} %param.11), kind=kOutput, calls=%fused_computation.20 | convolution fusion | flops 555745280 | bytes 13369344 | tf_op jit(solution)/shard_map/dot_general | solution.py:127
  318.7 2.2 convolution_add_fusion.1
  320.9 11.8 %fusion.18 = f32[128,1024]{1,0:T(8,128)} fusion(bf16[2048,128]{1,0:T(8,128)(2,1)} %bitcast.309, f32[2048,1024]{1,0:T(8,128)} %copy-done.5, bf16[2048,1024]{1,0:T(8,128)(2,1)} %multiply_convert_fusion.1, bf16[1024,1024]{1,0:T(8,128)(2,1)S(1)} %copy-done), kind=kOutput, calls=%fused_computation.51 | convolution fusion | flops 4850712576 | bytes 15728640 | tf_op jit(solution)/shard_map/dot_general | solution.py:134
  332.7 13.0 %convolution_add_fusion = f32[1024,1024]{1,0:T(8,128)} fusion(f32[1024,1024]{1,0:T(8,128)} %fusion.110, bf16[2048,1024]{1,0:T(8,128)(2,1)} %multiply_convert_fusion.1, f32[2048,1024]{1,0:T(8,128)} %copy-done.5), kind=kOutput, calls=%fused_computation.33 | convolution fusion | flops 4306501632 | bytes 20971520 | tf_op jit(solution)/shard_map/dot_general | solution.py:129
  345.7 1.5 convolution_add_fusion.2
  347.2 2.0 convolution_bitcast_fusion.9
  349.5 25.9 %all_to_all.120 = f32[1,8,64,2,128]{4,1,3,0,2:T(8,128)S(1)} all-to-all(f32[1,8,64,2,128]{4,1,3,0,2:T(8,128)S(1)} %copy.115), channel_id=1, replica_groups=mesh['lat'=16,'dp'=2] {'lat'}, dimensions={2} | all-to-all | bytes 1048576 | tf_op jit(solution)/shard_map/all_to_all | solution.py:98
  377.3 21.9 %all_to_all.121 = f32[1,128,4,2,128]{4,3,2,0,1:T(2,128)S(1)} all-to-all(f32[1,128,4,2,128]{4,3,2,0,1:T(2,128)S(1)} %copy.117), channel_id=1, replica_groups=mesh['lat'=16,'dp'=2] {'lat'}, dimensions={1} | all-to-all | bytes 1048576 | tf_op jit(solution)/shard_map/all_to_all | solution.py:104
  399.7 2.1 convolution_bitcast_fusion.2
  401.7 112.9 %all-reduce.3.cloned.1.call-done = (f32[128,1024]{1,0:T(8,128)}, f32[1024,1024]{1,0:T(8,128)}, f32[1024,128]{1,0:T(8,128)}) async-done(((f32[128,1024]{1,0:T(8,128)}, f32[1024,1024]{1,0:T(8,128)}, f32[1024,128]{1,0:T(8,128)}), (f32[128,1024]{1,0:T(8,128)}, f32[1024,1024]{1,0:T(8,128)}, f32[1024,128]{1,0:T(8,128)})) %all-reduce.3.cloned.1.call-update) | async-done | bytes 5242896 | tf_op jit(solution)/shard_map/psum | solution.py:138
  514.6 1.9 copy.186
  516.6 4.8 copy.187
  (581 shorter events, 145.2 us)
Async XLA Ops:
  7.2 148.9 %copy-start = (bf16[1024,1024]{1,0:T(8,128)(2,1)S(1)}, bf16[1024,1024]{1,0:T(8,128)(2,1)}, u32[]{:S(2)}) copy-start(bf16[1024,1024]{1,0:T(8,128)(2,1)} %param.10) | copy-start | bytes 6291460
  10.7 158.5 %all-to-all-start.4 = ((f32[1,8,64,2,128]{4,1,3,0,2:T(8,128)}), f32[1,8,64,2,128]{4,1,3,0,2:T(8,128)S(1)}, u32[]{:S(2)}, u32[]{:S(2)}) async-start(f32[1,8,64,2,128]{4,1,3,0,2:T(8,128)} %copy.120), calls=%async_computation.4 | async-start | bytes 1048576 | tf_op jit(solution)/shard_map/all_to_all | solution.py:98
  153.1 0.8 copy-start.7
  156.1 7.9 %copy-start.5 = (f32[2048,1024]{1,0:T(8,128)}, f32[2048,1024]{1,0:T(8,128)S(1)}, u32[]{:S(2)}) copy-start(f32[2048,1024]{1,0:T(8,128)S(1)} %fusion.108) | copy-start | bytes 25165828
  156.1 9.9 %copy-start.13 = (bf16[1024,128]{1,0:T(8,128)(2,1)S(1)}, bf16[1024,128]{1,0:T(8,128)(2,1)}, u32[]{:S(2)}) copy-start(bf16[1024,128]{1,0:T(8,128)(2,1)} %param.11) | copy-start | bytes 786436
  156.1 11.2 %copy-start.6 = (f32[1,8,256,128]{3,2,1,0:T(8,128)S(1)}, f32[1,8,256,128]{3,2,1,0:T(8,128)}, u32[]{:S(2)}) copy-start(f32[1,8,256,128]{3,2,1,0:T(8,128)} %param.7) | copy-start | bytes 3145732
  164.0 2.0 copy-start.1
  169.2 21.4 %all-to-all-start = ((f32[1,8,64,2,128]{4,1,3,0,2:T(8,128)}), f32[1,8,64,2,128]{4,1,3,0,2:T(8,128)S(1)}, u32[]{:S(2)}, u32[]{:S(2)}) async-start(f32[1,8,64,2,128]{4,1,3,0,2:T(8,128)} %copy.109), calls=%async_computation | async-start | bytes 1048576 | tf_op jit(solution)/shard_map/all_to_all | solution.py:98
  190.6 18.4 %all-to-all-start.5 = ((f32[1,128,4,2,128]{4,3,2,0,1:T(2,128)}), f32[1,128,4,2,128]{4,3,2,0,1:T(2,128)S(1)}, u32[]{:S(2)}, u32[]{:S(2)}) async-start(f32[1,128,4,2,128]{4,3,2,0,1:T(2,128)} %copy.122), calls=%async_computation.5 | async-start | bytes 1048576 | tf_op jit(solution)/shard_map/all_to_all | solution.py:104
  209.0 18.6 %all-to-all-start.1 = ((f32[1,128,4,2,128]{4,3,2,0,1:T(2,128)}), f32[1,128,4,2,128]{4,3,2,0,1:T(2,128)}, u32[]{:S(2)}, u32[]{:S(2)}) async-start(f32[1,128,4,2,128]{4,3,2,0,1:T(2,128)} %copy.112), calls=%async_computation.1 | async-start | bytes 1048576 | tf_op jit(solution)/shard_map/all_to_all | solution.py:104
  231.2 3.6 copy-start.10
  234.8 6.9 %copy-start.17 = (bf16[2048,1024]{1,0:T(8,128)(2,1)}, bf16[2048,1024]{1,0:T(8,128)(2,1)S(1)}, u32[]{:S(2)}) copy-start(bf16[2048,1024]{1,0:T(8,128)(2,1)S(1)} %get-tuple-element.221) | copy-start | bytes 12582916
  234.8 6.9 %copy-start.9 = (bf16[1,8,256,128]{3,2,1,0:T(8,128)(2,1)S(1)}, bf16[1,8,256,128]{3,2,1,0:T(8,128)(2,1)}, u32[]{:S(2)}) copy-start(bf16[1,8,256,128]{3,2,1,0:T(8,128)(2,1)} %get-tuple-element.225) | copy-start | bytes 1572868
  234.8 6.9 %copy-start.14 = (bf16[1024,128]{1,0:T(8,128)(2,1)S(1)}, bf16[1024,128]{1,0:T(8,128)(2,1)}, u32[]{:S(2)}) copy-start(bf16[1024,128]{1,0:T(8,128)(2,1)} %param.11) | copy-start | bytes 786436
  245.3 17.1 %copy-start.18 = (bf16[2048,1024]{1,0:T(8,128)(2,1)}, bf16[2048,1024]{1,0:T(8,128)(2,1)S(1)}, u32[]{:S(2)}) copy-start(bf16[2048,1024]{1,0:T(8,128)(2,1)S(1)} %multiply_convert_fusion.3) | copy-start | bytes 12582916
  245.3 19.1 %copy-start.12 = (bf16[128,1024]{1,0:T(8,128)(2,1)S(1)}, bf16[128,1024]{1,0:T(8,128)(2,1)}, u32[]{:S(2)}) copy-start(bf16[128,1024]{1,0:T(8,128)(2,1)} %param.9) | copy-start | bytes 786436
  262.4 2.0 copy-start.3
  267.6 18.1 %all-to-all-start.6 = ((f32[1,8,64,2,128]{4,1,3,0,2:T(8,128)}), f32[1,8,64,2,128]{4,1,3,0,2:T(8,128)}, u32[]{:S(2)}, u32[]{:S(2)}) async-start(f32[1,8,64,2,128]{4,1,3,0,2:T(8,128)} %copy.125), calls=%async_computation.6 | async-start | bytes 1048576 | tf_op jit(solution)/shard_map/all_to_all | solution.py:98
  291.1 17.8 %all-to-all-start.7 = ((f32[1,128,4,2,128]{4,3,2,0,1:T(2,128)}), f32[1,128,4,2,128]{4,3,2,0,1:T(2,128)}, u32[]{:S(2)}, u32[]{:S(2)}) async-start(f32[1,128,4,2,128]{4,3,2,0,1:T(2,128)} %copy.127), calls=%async_computation.7 | async-start | bytes 1048576 | tf_op jit(solution)/shard_map/all_to_all | solution.py:104
  295.4 219.3 %all-reduce.3.cloned.1.call-start = ((), (), s32[]{:S(2)}) async-start(), calls=%async_computation.8 | async-start | bytes 10485760 | tf_op jit(solution)/shard_map/psum | solution.py:138
  311.5 7.2 %copy-start.2 = (bf16[2048,1024]{1,0:T(8,128)(2,1)S(1)}, bf16[2048,1024]{1,0:T(8,128)(2,1)}, u32[]{:S(2)}) copy-start(bf16[2048,1024]{1,0:T(8,128)(2,1)} %copy-done.1) | copy-start | bytes 12582916
  311.5 7.2 %copy-start.8 = (f32[1024,128]{1,0:T(8,128)S(1)}, f32[1024,128]{1,0:T(8,128)}, u32[]{:S(2)}) copy-start(f32[1024,128]{1,0:T(8,128)} %fusion.111) | copy-start | bytes 1572868
  332.7 13.0 %copy-start.4 = (bf16[2048,1024]{1,0:T(8,128)(2,1)S(1)}, bf16[2048,1024]{1,0:T(8,128)(2,1)}, u32[]{:S(2)}) copy-start(bf16[2048,1024]{1,0:T(8,128)(2,1)} %copy-done.3) | copy-start | bytes 12582916
  332.7 13.0 %copy-start.11 = (bf16[1,8,256,128]{3,2,1,0:T(8,128)(2,1)S(1)}, bf16[1,8,256,128]{3,2,1,0:T(8,128)(2,1)}, u32[]{:S(2)}) copy-start(bf16[1,8,256,128]{3,2,1,0:T(8,128)(2,1)} %copy-done.10) | copy-start | bytes 1572868
  332.7 13.0 %copy-start.16 = (f32[128,1024]{1,0:T(8,128)S(1)}, f32[128,1024]{1,0:T(8,128)}, u32[]{:S(2)}) copy-start(f32[128,1024]{1,0:T(8,128)} %fusion.18) | copy-start | bytes 1572868
  514.6 6.7 %copy-start.15 = (f32[1024,128]{1,0:T(8,128)S(1)}, f32[1024,128]{1,0:T(8,128)}, u32[]{:S(2)}) copy-start(f32[1024,128]{1,0:T(8,128)} %get-tuple-element.306) | copy-start | bytes 1572868
Sparse Core Ops, SparseCore 0:
  347.4 167.2 all-reduce.2
where the time goes:
time: 540 us; the launch traced here: 529 us
  waiting for transfers between devices  158 us (29%)
  matrix products  118 us (22%)
  other arithmetic  93.3 us (17%)
  local copies, waits for them, and re-layouts  63.1 us (12%)
  blocking collectives  47.8 us (9%)
  starting transfers between devices  32.3 us (6%)
  between operations  15 us (3%)
    psum x1, waiting for transfers between devices, body(): lax.psum((total_first, total_middle, total_last), ('lat', 'dp'))  113 us
    while x63, other arithmetic  42.2 us
    sqrt x63, other arithmetic, advance(): jnp.sqrt((4.0 * degree * degree - 1.0) / (degree * degree - order_m * ord...  41.3 us
    dynamic_slice x63, local copies, waits for them, and re-layouts, legendre(): lax.scan(advance, initial, jnp.arange(1, wave_count).astype(jnp.float32))  36.9 us
    all_to_all x3, waiting for transfers between devices, spectral(): lax.all_to_all(back_grid, 'lat', split_axis=1, concat_axis=2, tiled=True)  27 us
    all_to_all x1, blocking collectives, spectral(): lax.all_to_all(wave_grid, 'lat', split_axis=2, concat_axis=1, tiled=True)  25.9 us
    dot_general x2, matrix products, body(): jnp.dot(hidden_first.T, middle_grad, preferred_element_type=jnp.float32)  23.1 us
    all_to_all x1, blocking collectives, spectral(): lax.all_to_all(back_grid, 'lat', split_axis=1, concat_axis=2, tiled=True)  21.9 us
  transfers between devices with their start and end apart: 7, of which 6 were waited for; matrix products, arithmetic and copies ran while one was open for 33% of the time, Pallas kernels for 0%

commit v1 on v0

v1 whole, which is shorter than its diff:
```python
import functools
import math

import jax
import jax.numpy as jnp
import numpy as np
from jax import lax
from jax.experimental import pallas as pl
from jax.experimental.pallas import tpu as pltpu
from jax.sharding import PartitionSpec as P

MW = 64
STEPS = 2

high = lax.Precision.HIGH
tend_weight = 0.5


def grid_tables(lon_count, wave_count):
    lon_index = np.arange(lon_count)
    wave_index = np.arange(wave_count)
    angle = 2.0 * math.pi * (lon_index[:, None] * wave_index[None, :] % lon_count) / lon_count
    pair = np.stack([np.cos(angle), -np.sin(angle)], axis=2)
    factor = np.where(wave_index == 0, 1.0, 2.0)
    analysis = (pair / lon_count).reshape(lon_count, -1).astype(np.float32)
    synthesis = (pair * factor[None, :, None]).reshape(lon_count, -1).astype(np.float32)
    return analysis, synthesis


def legendre_tables(lat_count, wave_count):
    latitude = -0.5 * math.pi + (np.arange(lat_count) + 0.5) * math.pi / lat_count
    mu, cosine = np.sin(latitude), np.cos(latitude)
    quad_weight = cosine * math.pi / lat_count
    order = np.arange(wave_count, dtype=np.float64)
    steps = np.concatenate([[0.0], 0.5 * np.log((2 * order[1:] + 1) / (2 * order[1:]))])
    diagonal = np.exp(
        0.5 * math.log(0.5) + np.cumsum(steps)[:, None] + order[:, None] * np.log(cosine)[None, :]
    )
    rows = [diagonal]
    previous, current, ratio_prev = np.zeros_like(diagonal), diagonal, np.ones_like(order)
    for offset in range(1, wave_count):
        n = order + offset
        ratio = np.sqrt((4 * n * n - 1) / (n * n - order * order))
        following = ratio[:, None] * (mu[None, :] * current - previous / ratio_prev[:, None])
        previous, current, ratio_prev = current, following, ratio
        rows.append(following)
    table = np.stack(rows, axis=1)
    degree = order[:, None] + np.arange(wave_count)[None, :]
    kept = degree <= wave_count - 1
    damping = np.where(kept, 1.0 / (1.0 + degree * (degree + 1) / (wave_count * (wave_count - 1.0))), 0.0)
    table = np.where(kept[:, :, None], table, 0.0) * np.sqrt(damping)[:, :, None]
    return table.astype(np.float32), quad_weight.astype(np.float32)


def silu_pair(value):
    gate = 0.5 * jnp.tanh(0.5 * value) + 0.5
    hidden = value * gate
    return hidden, gate + hidden - hidden * gate


def forward_kernel(x_ref, w1_ref, w2_ref, w3_ref, moved_ref, h1_ref, s1_ref, h2_ref, s2_ref):
    field = x_ref[...]
    rows = field.astype(jnp.bfloat16)
    h1, s1 = silu_pair(jnp.dot(rows, w1_ref[...], preferred_element_type=jnp.float32))
    h1 = h1.astype(jnp.bfloat16)
    h1_ref[...] = h1
    s1_ref[...] = s1.astype(jnp.bfloat16)
    h2, s2 = silu_pair(jnp.dot(h1, w2_ref[...], preferred_element_type=jnp.float32))
    h2 = h2.astype(jnp.bfloat16)
    h2_ref[...] = h2
    s2_ref[...] = s2.astype(jnp.bfloat16)
    tend = jnp.dot(h2, w3_ref[...], preferred_element_type=jnp.float32)
    moved_ref[...] = field + tend_weight * tend


def forward_rows(x, w1, w2, w3):
    count, features = x.shape
    hidden = w1.shape[1]
    tile = math.gcd(count, 256)
    row = lambda width: pl.BlockSpec((tile, width), lambda i: (i, 0))
    whole = lambda w: pl.BlockSpec(w.shape, lambda i: (0, 0))
    wide = jax.ShapeDtypeStruct((count, hidden), jnp.bfloat16)
    return pl.pallas_call(
        forward_kernel,
        grid=(count // tile,),
        in_specs=[row(features), whole(w1), whole(w2), whole(w3)],
        out_specs=[row(features)] + [row(hidden)] * 4,
        out_shape=[jax.ShapeDtypeStruct(x.shape, jnp.float32)] + [wide] * 4,
        cost_estimate=pl.CostEstimate(
            flops=2 * count * (2 * features * hidden + hidden * hidden),
            bytes_accessed=count * hidden * 8, transcendentals=2 * count * hidden,
        ),
        compiler_params=pltpu.CompilerParams(dimension_semantics=("arbitrary",)),
    )(x, w1, w2, w3)


def mul_t(a, b):
    return lax.dot_general(a, b, (((1,), (1,)), ((), ())), preferred_element_type=jnp.float32)


def t_mul(a, b):
    return lax.dot_general(a, b, (((0,), (0,)), ((), ())), preferred_element_type=jnp.float32)


def backward_kernel(first_call, need_rows, *refs):
    p_ref, x_ref, h1_ref, s1_ref, h2_ref, s2_ref, w1_ref, w2_ref, w3_ref = refs[:9]
    refs = refs[9:]
    if not first_call:
        c1_ref, c2_ref, c3_ref = refs[:3]
        refs = refs[3:]
    g1_ref, g2_ref, g3_ref = refs[:3]

    @pl.when(pl.program_id(0) == 0)
    def _():
        if first_call:
            g1_ref[...] = jnp.zeros_like(g1_ref)
            g2_ref[...] = jnp.zeros_like(g2_ref)
            g3_ref[...] = jnp.zeros_like(g3_ref)
        else:
            g1_ref[...] = c1_ref[...]
            g2_ref[...] = c2_ref[...]
            g3_ref[...] = c3_ref[...]

    pulled = p_ref[...]
    gt = (tend_weight * pulled).astype(jnp.bfloat16)
    g3_ref[...] += t_mul(h2_ref[...], gt)
    ga2 = (mul_t(gt, w3_ref[...]) * s2_ref[...].astype(jnp.float32)).astype(jnp.bfloat16)
    g2_ref[...] += t_mul(h1_ref[...], ga2)
    ga1 = (mul_t(ga2, w2_ref[...]) * s1_ref[...].astype(jnp.float32)).astype(jnp.bfloat16)
    g1_ref[...] += t_mul(x_ref[...].astype(jnp.bfloat16), ga1)
    if need_rows:
        refs[3][...] = pulled + mul_t(ga1, w1_ref[...])


def backward_rows(pulled, x, saved, w1, w2, w3, carry, need_rows):
    count, features = x.shape
    hidden = w1.shape[1]
    tile = math.gcd(count, 512)
    row = lambda width: pl.BlockSpec((tile, width), lambda i: (i, 0))
    whole = lambda w: pl.BlockSpec(w.shape, lambda i: (0, 0))
    out_shape = [jax.ShapeDtypeStruct(w.shape, jnp.float32) for w in (w1, w2, w3)]
    out_specs = [whole(w) for w in (w1, w2, w3)]
    carried = [] if carry is None else list(carry)
    if need_rows:
        out_shape.append(jax.ShapeDtypeStruct(x.shape, jnp.float32))
        out_specs.append(row(features))
    return pl.pallas_call(
        functools.partial(backward_kernel, carry is None, need_rows),
        grid=(count // tile,),
        in_specs=[row(features)] * 2 + [row(hidden)] * 4
        + [whole(w) for w in (w1, w2, w3)] + [whole(c) for c in carried],
        out_specs=out_specs,
        out_shape=out_shape,
        cost_estimate=pl.CostEstimate(
            flops=4 * count * (2 * features * hidden + hidden * hidden),
            bytes_accessed=count * hidden * 8, transcendentals=0,
        ),
        compiler_params=pltpu.CompilerParams(dimension_semantics=("arbitrary",)),
    )(pulled, x, *saved, w1, w2, w3, *carried)


def body(state, cotangent, w1, w2, w3):
    sample, lat_rows, lon_count, features = state.shape
    bands = lax.axis_size("lat")
    lat_count = lat_rows * bands
    waves = MW // bands
    analysis, synthesis = grid_tables(lon_count, MW)
    table, quad = legendre_tables(lat_count, MW)
    mine = lax.dynamic_slice_in_dim(jnp.asarray(table), lax.axis_index("lat") * waves, waves, axis=0)
    base = jnp.einsum("mki,mkj->mij", mine, mine, precision=lax.Precision.HIGHEST)
    quad = jnp.asarray(quad)
    forward_op = base * quad[None, None, :]
    backward_op = base * quad[None, :, None]

    def spectral(parts):
        sent = []
        for field, first, _, _ in parts:
            wav = jnp.einsum("bjxf,xq->bqjf", field, first, precision=high)
            sent.append(wav.reshape(sample, bands, waves * 2, lat_rows, features))
        sent = jnp.concatenate(sent, axis=0).transpose(1, 0, 2, 3, 4)
        got = lax.all_to_all(sent, "lat", split_axis=0, concat_axis=0, tiled=True)
        got = got.reshape(bands, len(parts), sample, waves, 2, lat_rows, features)
        ops = jnp.stack([p[2] for p in parts]).reshape(len(parts), waves, bands, lat_rows, lat_count)
        got = got.transpose(1, 3, 0, 5, 2, 4, 6).reshape(len(parts), waves, lat_count, -1)
        ops = ops.reshape(len(parts), waves, lat_count, lat_count)
        back = jnp.einsum("smij,smjv->smiv", ops, got, precision=high)
        back = back.reshape(len(parts), waves, bands, lat_rows, sample, 2, features)
        back = back.transpose(2, 0, 4, 1, 5, 3, 6)
        back = lax.all_to_all(back, "lat", split_axis=0, concat_axis=0, tiled=True)
        out = []
        for index, (_, _, _, last) in enumerate(parts):
            piece = back[:, index].transpose(1, 0, 2, 3, 4, 5)
            piece = piece.reshape(sample, MW * 2, lat_rows, features)
            out.append(jnp.einsum("bqjf,xq->bjxf", piece, last, precision=high))
        return out

    flat = lambda field: field.reshape(sample * lat_rows * lon_count, features)
    x0 = flat(state)
    moved0, *saved0 = forward_rows(x0, w1, w2, w3)
    q1, pulled1 = spectral([
        (moved0.reshape(state.shape), analysis, forward_op, synthesis),
        (cotangent, synthesis, backward_op, analysis),
    ])
    x1 = flat(q1)
    moved1, *saved1 = forward_rows(x1, w1, w2, w3)
    *totals, grad = backward_rows(flat(pulled1), x1, saved1, w1, w2, w3, None, True)
    final, pulled0 = spectral([
        (moved1.reshape(state.shape), analysis, forward_op, synthesis),
        (grad.reshape(state.shape), synthesis, backward_op, analysis),
    ])
    totals = backward_rows(flat(pulled0), x0, saved0, w1, w2, w3, totals, False)
    totals = reduce_totals(totals)
    return (final, *totals)


def reduce_totals(totals):
    return lax.psum(tuple(totals), ("lat", "dp"))


def solution(mesh):
    field = P("dp", "lat", None, None)
    return jax.shard_map(
        body, mesh=mesh, in_specs=(field, field, P(), P(), P()),
        out_specs=(field, P(), P(), P()), check_vma=False,
    )
```

time: 540 us -> 372 us (0.69); the launches traced: 529 us -> 372 us
  matrix products: 118 us -> 15.5 us
  other arithmetic: 93.3 us -> 0.16 us
  Pallas kernels: 0 us -> 65.7 us
  local copies, waits for them, and re-layouts: 63.1 us -> 11.6 us
  blocking collectives: 47.8 us -> 88.1 us
  starting transfers between devices: 32.3 us -> 8.38 us
  waiting for transfers between devices: 158 us -> 168 us
    dot_general x32 -> x11, matrix products: 118 us -> 15.5 us  [the longest x4 6.23 us: spectral(): wav = jnp.einsum('bjxf,xq->bqjf', field, first, precision=high)]
    pallas_call x0 -> x4, Pallas kernels: none -> 65.7 us  [the longest x2 37.4 us: backward_rows(): pl.pallas_call(functools.partial(backward_kernel, carry is None, need_row...]
    while x63 -> x0, other arithmetic: 42.2 us -> none
    sqrt x63 -> x0, other arithmetic: 41.3 us -> none  [advance(): jnp.sqrt((4.0 * degree * degree - 1.0) / (degree * degree - order_m * ord...]
    all_to_all x2 -> x3, blocking collectives: 47.8 us -> 88.1 us  [the longest x2 59.4 us: spectral(): back = lax.all_to_all(back, 'lat', split_axis=0, concat_axis=0, tiled=True)]
    dynamic_slice x63 -> x0, local copies, waits for them, and re-layouts: 36.9 us -> none  [legendre(): lax.scan(advance, initial, jnp.arange(1, wave_count).astype(jnp.float32))]
    psum x1, waiting for transfers between devices: 113 us -> 145 us  [reduce_totals(): return lax.psum(tuple(totals), ('lat', 'dp'))]
    all_to_all x6 -> x1, starting transfers between devices: 32.2 us -> 8.34 us  [spectral(): got = lax.all_to_all(sent, 'lat', split_axis=0, concat_axis=0, tiled=True)]
  transfers between devices with their start and end apart: 7 -> 2, of which waited for: 6 -> 2; matrix products, arithmetic and copies ran while one was open for 33% -> 1% of each run, Pallas kernels for 0% -> 0%
where the time goes in v1:
time: 372 us
  waiting for transfers between devices  168 us (45%)
  blocking collectives  88.1 us (24%)
  Pallas kernels  65.7 us (18%)
  matrix products  15.5 us (4%)
  between operations  14.3 us (4%)
  local copies, waits for them, and re-layouts  11.6 us (3%)
  starting transfers between devices  8.38 us (2%)
    psum x1, waiting for transfers between devices, reduce_totals(): return lax.psum(tuple(totals), ('lat', 'dp'))  145 us
    all_to_all x2, blocking collectives, spectral(): back = lax.all_to_all(back, 'lat', split_axis=0, concat_axis=0, tiled=True)  59.4 us
    pallas_call x2, Pallas kernels, backward_rows(): pl.pallas_call(functools.partial(backward_kernel, carry is None, need_row...  37.4 us
    all_to_all x1, blocking collectives, spectral(): got = lax.all_to_all(sent, 'lat', split_axis=0, concat_axis=0, tiled=True)  28.7 us
    pallas_call x2, Pallas kernels, forward_rows(): pl.pallas_call(forward_kernel, grid=(count // tile,), in_specs=[row(featu...  28.4 us
    all_to_all x1, waiting for transfers between devices, spectral(): got = lax.all_to_all(sent, 'lat', split_axis=0, concat_axis=0, tiled=True)  22.7 us
    unnamed x19, local copies, waits for them, and re-layouts  8.87 us
    all_to_all x1, starting transfers between devices, spectral(): got = lax.all_to_all(sent, 'lat', split_axis=0, concat_axis=0, tiled=True)  8.34 us
  transfers between devices with their start and end apart: 2, of which 2 were waited for; matrix products, arithmetic and copies ran while one was open for 1% of the time, Pallas kernels for 0%

profile of v1, /device:TPU:0, one launch (start us, length us, event | category | flops | bytes accessed | tf_op | source)
XLA Modules:
  0.0 371.7 jit_solution(15232433059005781025)
XLA Ops:
  7.2 0.0 copy-start
  7.2 1.2 copy-done
  8.4 1.3 convolution_bitcast_fusion.5
  9.7 0.0 copy-start.6
  9.7 14.2 %shard_map.174 = (f32[2048,128]{1,0:T(8,128)}, bf16[2048,1024]{1,0:T(8,128)(2,1)}, bf16[2048,1024]{1,0:T(8,128)(2,1)}, bf16[2048,1024]{1,0:T(8,128)(2,1)}, bf16[2048,1024]{1,0:T(8,128)(2,1)}) custom-call(f32[2048,128]{1,0:T(8,128)} %bitcast.113, bf16[128,1024]{1,0:T(8,128)(2,1)} %refs_6_.3, bf16[1024,1024]{1,0:T(8,128)(2,1)} %refs_7_.3, ...), custom_call_target="tpu_custom_call" | custom-call | flops 5368709120 | bytes 16777216 | tf_op jit(solution)/shard_map/pallas_call | solution.py:83
  23.9 0.0 copy-start.7
  23.9 0.0 copy-done.6
  24.0 1.6 convolution_bitcast_fusion.6
  25.6 0.1 maximum_bitcast_fusion
  25.7 1.1 copy.25
  26.8 8.3 %all-to-all-start = ((f32[16,2,8,8,128]{4,2,3,1,0:T(8,128)}), f32[16,2,8,8,128]{4,2,3,1,0:T(8,128)S(1)}, u32[]{:S(2)}, u32[]{:S(2)}) async-start(f32[16,2,8,8,128]{4,2,3,1,0:T(8,128)} %copy.25), calls=%async_computation | async-start | bytes 2097152 | tf_op jit(solution)/shard_map/all_to_all | solution.py:181
  35.1 0.0 all-reduce.3.cloned.1.call-start
  35.2 0.0 copy-done.7
  35.2 1.6 multiply_bitcast_fusion.1
  36.8 22.7 %all-to-all-done = f32[16,2,8,8,128]{4,2,3,1,0:T(8,128)S(1)} async-done(((f32[16,2,8,8,128]{4,2,3,1,0:T(8,128)}), f32[16,2,8,8,128]{4,2,3,1,0:T(8,128)S(1)}, u32[]{:S(2)}, u32[]{:S(2)}) %all-to-all-start) | async-done | bytes 1048608 | tf_op jit(solution)/shard_map/all_to_all | solution.py:181
  59.5 0.7 convolution_bitcast_fusion.2
  60.3 0.0 copy-start.3
  60.3 0.1 copy.48
  60.4 30.7 %all_to_all.20 = f32[16,2,1,4,2,8,128]{6,5,4,3,1,2,0:T(8,128)S(1)} all-to-all(f32[16,2,1,4,2,8,128]{6,5,4,3,1,2,0:T(8,128)S(1)} %bitcast.100), channel_id=1, replica_groups=mesh['lat'=16,'dp'=2] {'lat'}, dimensions={0} | all-to-all | bytes 2097152 | tf_op jit(solution)/shard_map/all_to_all | solution.py:189
  91.1 0.1 fusion.11
  91.2 0.3 copy.28
  91.5 0.3 copy.29
  91.7 0.0 copy-done.3
  91.8 1.6 fusion.14
  93.3 14.2 %shard_map.175 = (f32[2048,128]{1,0:T(8,128)}, bf16[2048,1024]{1,0:T(8,128)(2,1)}, bf16[2048,1024]{1,0:T(8,128)(2,1)}, bf16[2048,1024]{1,0:T(8,128)(2,1)}, bf16[2048,1024]{1,0:T(8,128)(2,1)}) custom-call(f32[2048,128]{1,0:T(8,128)} %bitcast.106, bf16[128,1024]{1,0:T(8,128)(2,1)} %refs_6_.3, bf16[1024,1024]{1,0:T(8,128)(2,1)} %refs_7_.3, ...), custom_call_target="tpu_custom_call" | custom-call | flops 5368709120 | bytes 16777216 | tf_op jit(solution)/shard_map/pallas_call | solution.py:83
  107.5 1.6 convolution_bitcast_fusion.4
  109.2 0.0 copy-done.4
  109.2 1.5 fusion.15
  110.7 18.3 %shard_map.176 = (f32[128,1024]{1,0:T(8,128)}, f32[1024,1024]{1,0:T(8,128)}, f32[1024,128]{1,0:T(8,128)}, f32[2048,128]{1,0:T(8,128)}) custom-call(f32[2048,128]{1,0:T(8,128)} %bitcast.109, f32[2048,128]{1,0:T(8,128)} %bitcast.107, bf16[2048,1024]{1,0:T(8,128)(2,1)} %get-tuple-element.23.refs_2_, bf16[2048,1024]{1,0:T(8,128)(2,1)} %get-tuple-element.24.refs_3_, ...), custom_call_target="tpu_custom_call" | custom-call | flops 10737418240 | bytes 16777216 | tf_op jit(solution)/shard_map/pallas_call | solution.py:147
  129.1 1.6 convolution_bitcast_fusion.3
  130.7 0.1 maximum_bitcast_fusion.1
  130.8 0.1 copy.30
  130.9 28.7 %all_to_all.21 = f32[16,2,8,8,128]{4,2,3,1,0:T(8,128)S(1)} all-to-all(f32[16,2,8,8,128]{4,2,3,1,0:T(8,128)S(1)} %copy.30), channel_id=1, replica_groups=mesh['lat'=16,'dp'=2] {'lat'}, dimensions={0} | all-to-all | bytes 2097152 | tf_op jit(solution)/shard_map/all_to_all | solution.py:181
  159.6 0.7 convolution_bitcast_fusion.1
  160.3 0.1 copy.47
  160.5 28.7 %all_to_all.22 = f32[16,2,1,4,2,8,128]{6,5,4,3,1,2,0:T(8,128)S(1)} all-to-all(f32[16,2,1,4,2,8,128]{6,5,4,3,1,2,0:T(8,128)S(1)} %bitcast.101), channel_id=1, replica_groups=mesh['lat'=16,'dp'=2] {'lat'}, dimensions={0} | all-to-all | bytes 2097152 | tf_op jit(solution)/shard_map/all_to_all | solution.py:189
  189.2 0.1 fusion.10
  189.3 0.3 copy.34
  189.6 1.5 fusion.16
  191.1 19.0 %shard_map.177 = (f32[128,1024]{1,0:T(8,128)}, f32[1024,1024]{1,0:T(8,128)}, f32[1024,128]{1,0:T(8,128)}) custom-call(f32[2048,128]{1,0:T(8,128)} %bitcast.108, f32[2048,128]{1,0:T(8,128)} %bitcast.114, bf16[2048,1024]{1,0:T(8,128)(2,1)} %get-tuple-element.28.refs_2_, bf16[2048,1024]{1,0:T(8,128)(2,1)} %get-tuple-element.29.refs_3_, ...), custom_call_target="tpu_custom_call" | custom-call | flops 10737418240 | bytes 16777216 | tf_op jit(solution)/shard_map/pallas_call | solution.py:147
  210.2 0.0 all-reduce.3.cloned.1.call-update
  210.2 0.3 copy.33
  210.5 1.5 convolution_bitcast_fusion
  212.0 145.2 %all-reduce.3.cloned.1.call-done = (f32[128,1024]{1,0:T(8,128)}, f32[1024,1024]{1,0:T(8,128)}, f32[1024,128]{1,0:T(8,128)}) async-done(((f32[128,1024]{1,0:T(8,128)}, f32[1024,1024]{1,0:T(8,128)}, f32[1024,128]{1,0:T(8,128)}), (f32[128,1024]{1,0:T(8,128)}, f32[1024,1024]{1,0:T(8,128)}, f32[1024,128]{1,0:T(8,128)})) %all-reduce.3.cloned.1.call-update) | async-done | bytes 5242896 | tf_op jit(solution)/shard_map/psum | solution.py:217
  357.2 2.0 copy.52
  359.2 4.8 %copy.53 = f32[1024,1024]{1,0:T(8,128)} copy(f32[1024,1024]{1,0:T(8,128)} %get-tuple-element.49) | data formatting | bytes 8388608
  364.0 0.8 copy.54
  364.8 0.0 copy-done.1
  (6 shorter events, 0.0 us)
Async XLA Ops:
  7.2 1.2 copy-start
  9.7 14.2 %copy-start.6 = (f32[16,8,256,1]{2,1,3,0:T(8,128)S(1)}, f32[16,8,256,1]{2,1,3,0:T(8,128)}, u32[]{:S(2)}) copy-start(f32[16,8,256,1]{2,1,3,0:T(8,128)} %constant.31) | copy-start | bytes 393220
  23.9 11.3 %copy-start.7 = (f32[128]{0:T(128)S(1)}, f32[128]{0:T(128)}, u32[]{:S(2)}) copy-start(f32[128]{0:T(128)} %constant.21.clone) | copy-start | bytes 1540
  26.8 32.7 %all-to-all-start = ((f32[16,2,8,8,128]{4,2,3,1,0:T(8,128)}), f32[16,2,8,8,128]{4,2,3,1,0:T(8,128)S(1)}, u32[]{:S(2)}, u32[]{:S(2)}) async-start(f32[16,2,8,8,128]{4,2,3,1,0:T(8,128)} %copy.25), calls=%async_computation | async-start | bytes 2097152 | tf_op jit(solution)/shard_map/all_to_all | solution.py:181
  35.1 322.1 %all-reduce.3.cloned.1.call-start = ((), (), s32[]{:S(2)}) async-start(), calls=%async_computation.4 | async-start | bytes 10485760 | tf_op jit(solution)/shard_map/psum | solution.py:217
  60.3 31.5 %copy-start.3 = (f32[256,128,1]{1,0,2:T(8,128)S(1)}, f32[256,128,1]{1,0,2:T(8,128)}, u32[]{:S(2)}) copy-start(f32[256,128,1]{1,0,2:T(8,128)} %constant.30) | copy-start | bytes 393220
  93.3 15.8 %copy-start.4 = (f32[256,128,1]{1,0,2:T(8,128)S(1)}, f32[256,128,1]{1,0,2:T(8,128)}, u32[]{:S(2)}) copy-start(f32[256,128,1]{1,0,2:T(8,128)} %constant.33) | copy-start | bytes 393220
  110.7 18.3 %copy-start.5 = (f32[16,8,256,1]{2,1,3,0:T(8,128)S(1)}, f32[16,8,256,1]{2,1,3,0:T(8,128)}, u32[]{:S(2)}) copy-start(f32[16,8,256,1]{2,1,3,0:T(8,128)} %constant.32) | copy-start | bytes 393220
  357.2 7.6 %copy-start.1 = (f32[1,8,256,128]{3,2,1,0:T(8,128)S(1)}, f32[1,8,256,128]{3,2,1,0:T(8,128)}, u32[]{:S(2)}) copy-start(f32[1,8,256,128]{3,2,1,0:T(8,128)} %param.16) | copy-start | bytes 3145732
  359.2 4.8 %copy-start.2 = (f32[1024,128]{1,0:T(8,128)S(1)}, f32[1024,128]{1,0:T(8,128)}, u32[]{:S(2)}) copy-start(f32[1024,128]{1,0:T(8,128)} %get-tuple-element.50) | copy-start | bytes 1572868
Sparse Core Ops, SparseCore 0:
  210.3 146.8 all-reduce.2

commit v2 on v1

--- a/solution.py
+++ b/solution.py
@@ -197,17 +197,13 @@
     flat = lambda field: field.reshape(sample * lat_rows * lon_count, features)
     x0 = flat(state)
     moved0, *saved0 = forward_rows(x0, w1, w2, w3)
-    q1, pulled1 = spectral([
-        (moved0.reshape(state.shape), analysis, forward_op, synthesis),
-        (cotangent, synthesis, backward_op, analysis),
-    ])
+    (pulled1,) = spectral([(cotangent, synthesis, backward_op, analysis)])
+    (q1,) = spectral([(moved0.reshape(state.shape), analysis, forward_op, synthesis)])
     x1 = flat(q1)
     moved1, *saved1 = forward_rows(x1, w1, w2, w3)
     *totals, grad = backward_rows(flat(pulled1), x1, saved1, w1, w2, w3, None, True)
-    final, pulled0 = spectral([
-        (moved1.reshape(state.shape), analysis, forward_op, synthesis),
-        (grad.reshape(state.shape), synthesis, backward_op, analysis),
-    ])
+    (final,) = spectral([(moved1.reshape(state.shape), analysis, forward_op, synthesis)])
+    (pulled0,) = spectral([(grad.reshape(state.shape), synthesis, backward_op, analysis)])
     totals = backward_rows(flat(pulled0), x0, saved0, w1, w2, w3, totals, False)
     totals = reduce_totals(totals)
     return (final, *totals)

time: 372 us -> 368 us (0.989)
  waiting for transfers between devices: 168 us -> 153 us
  starting transfers between devices: 8.38 us -> 20.1 us
    psum x1, waiting for transfers between devices: 145 us -> 115 us  [reduce_totals(): return lax.psum(tuple(totals), ('lat', 'dp'))]
    all_to_all x2, blocking collectives: 59.4 us -> 40 us  [spectral(): back = lax.all_to_all(back, 'lat', split_axis=0, concat_axis=0, tiled=True)]
    all_to_all x1 -> x2, blocking collectives: 28.7 us -> 46.4 us  [spectral(): got = lax.all_to_all(sent, 'lat', split_axis=0, concat_axis=0, tiled=True)]
    all_to_all x0 -> x2, waiting for transfers between devices: none -> 13.1 us  [spectral(): back = lax.all_to_all(back, 'lat', split_axis=0, concat_axis=0, tiled=True)]
    all_to_all x0 -> x2, starting transfers between devices: none -> 7.74 us  [spectral(): back = lax.all_to_all(back, 'lat', split_axis=0, concat_axis=0, tiled=True)]
    all_to_all x1 -> x2, starting transfers between devices: 8.34 us -> 12.3 us  [spectral(): got = lax.all_to_all(sent, 'lat', split_axis=0, concat_axis=0, tiled=True)]
    all_to_all x1 -> x2, waiting for transfers between devices: 22.7 us -> 25.3 us  [spectral(): got = lax.all_to_all(sent, 'lat', split_axis=0, concat_axis=0, tiled=True)]
    unnamed x19 -> x21, local copies, waits for them, and re-layouts: 8.87 us -> 8.85 us
  transfers between devices with their start and end apart: 2 -> 5, of which waited for: 2 -> 4; matrix products, arithmetic and copies ran while one was open for 1% -> 3% of each run, Pallas kernels for 0% -> 4%
where the time goes in v2:
time: 368 us; the launch traced here: 367 us
  waiting for transfers between devices  153 us (42%)
  blocking collectives  86.4 us (23%)
  Pallas kernels  65.9 us (18%)
  starting transfers between devices  20.1 us (5%)
  matrix products  15.3 us (4%)
  between operations  14.3 us (4%)
  local copies, waits for them, and re-layouts  11.7 us (3%)
    psum x1, waiting for transfers between devices, reduce_totals(): return lax.psum(tuple(totals), ('lat', 'dp'))  115 us
    all_to_all x2, blocking collectives, spectral(): got = lax.all_to_all(sent, 'lat', split_axis=0, concat_axis=0, tiled=True)  46.4 us
    all_to_all x2, blocking collectives, spectral(): back = lax.all_to_all(back, 'lat', split_axis=0, concat_axis=0, tiled=True)  40 us
    pallas_call x2, Pallas kernels, backward_rows(): pl.pallas_call(functools.partial(backward_kernel, carry is None, need_row...  37.3 us
    pallas_call x2, Pallas kernels, forward_rows(): pl.pallas_call(forward_kernel, grid=(count // tile,), in_specs=[row(featu...  28.5 us
    all_to_all x2, waiting for transfers between devices, spectral(): got = lax.all_to_all(sent, 'lat', split_axis=0, concat_axis=0, tiled=True)  25.3 us
    all_to_all x2, waiting for transfers between devices, spectral(): back = lax.all_to_all(back, 'lat', split_axis=0, concat_axis=0, tiled=True)  13.1 us
    all_to_all x2, starting transfers between devices, spectral(): got = lax.all_to_all(sent, 'lat', split_axis=0, concat_axis=0, tiled=True)  12.3 us
  transfers between devices with their start and end apart: 5, of which 4 were waited for; matrix products, arithmetic and copies ran while one was open for 3% of the time, Pallas kernels for 4%

profile of v2, /device:TPU:0, one launch (start us, length us, event | category | flops | bytes accessed | tf_op | source)
XLA Modules:
  0.0 367.0 jit_solution(12545072260195943032)
XLA Ops:
  7.2 0.0 copy-start
  7.2 0.0 copy-start.5
  7.2 0.0 copy-start.7
  7.2 14.3 %shard_map.174 = (f32[2048,128]{1,0:T(8,128)}, bf16[2048,1024]{1,0:T(8,128)(2,1)}, bf16[2048,1024]{1,0:T(8,128)(2,1)}, bf16[2048,1024]{1,0:T(8,128)(2,1)}, bf16[2048,1024]{1,0:T(8,128)(2,1)}) custom-call(f32[2048,128]{1,0:T(8,128)} %bitcast.137, bf16[128,1024]{1,0:T(8,128)(2,1)} %refs_6_.3, bf16[1024,1024]{1,0:T(8,128)(2,1)} %refs_7_.3, ...), custom_call_target="tpu_custom_call" | custom-call | flops 5368709120 | bytes 16777216 | tf_op jit(solution)/shard_map/pallas_call | solution.py:83
  21.5 0.0 copy-start.8
  21.5 0.0 copy-done.5
  21.5 2.4 convolution_bitcast_fusion.8
  23.9 8.3 %all-to-all-start = ((f32[16,1,8,8,128]{4,2,3,1,0:T(8,128)}), f32[16,1,8,8,128]{4,2,3,1,0:T(8,128)S(1)}, u32[]{:S(2)}, u32[]{:S(2)}) async-start(f32[16,1,8,8,128]{4,2,3,1,0:T(8,128)} %convolution_bitcast_fusion.8), calls=%async_computation | async-start | bytes 1048576 | tf_op jit(solution)/shard_map/all_to_all | solution.py:181
  32.3 1.2 convolution_bitcast_fusion.4
  33.5 13.8 %all-to-all-done = f32[16,1,8,8,128]{4,2,3,1,0:T(8,128)S(1)} async-done(((f32[16,1,8,8,128]{4,2,3,1,0:T(8,128)}), f32[16,1,8,8,128]{4,2,3,1,0:T(8,128)S(1)}, u32[]{:S(2)}, u32[]{:S(2)}) %all-to-all-start) | async-done | bytes 524320 | tf_op jit(solution)/shard_map/all_to_all | solution.py:181
  47.4 3.9 %all-to-all-start.4 = ((f32[16,1,8,8,128]{4,2,3,1,0:T(8,128)}), f32[16,1,8,8,128]{4,2,3,1,0:T(8,128)S(1)}, u32[]{:S(2)}, u32[]{:S(2)}) async-start(f32[16,1,8,8,128]{4,2,3,1,0:T(8,128)} %convolution_bitcast_fusion.4), calls=%async_computation.4 | async-start | bytes 1048576 | tf_op jit(solution)/shard_map/all_to_all | solution.py:181
  51.3 0.0 copy-start.4
  51.3 1.6 fusion.17
  53.0 0.4 convolution_bitcast_fusion.7
  53.4 0.8 copy.68
  54.2 11.5 %all-to-all-done.4 = f32[16,1,8,8,128]{4,2,3,1,0:T(8,128)S(1)} async-done(((f32[16,1,8,8,128]{4,2,3,1,0:T(8,128)}), f32[16,1,8,8,128]{4,2,3,1,0:T(8,128)S(1)}, u32[]{:S(2)}, u32[]{:S(2)}) %all-to-all-start.4) | async-done | bytes 524320 | tf_op jit(solution)/shard_map/all_to_all | solution.py:181
  65.7 3.9 %all-to-all-start.1 = ((f32[16,1,1,4,2,8,128]{6,5,4,3,2,1,0:T(8,128)}), f32[16,1,1,4,2,8,128]{6,5,4,3,2,1,0:T(8,128)S(1)}, u32[]{:S(2)}, u32[]{:S(2)}) async-start(f32[16,1,1,4,2,8,128]{6,5,4,3,2,1,0:T(8,128)} %bitcast.119), calls=%async_computation.1 | async-start | bytes 1048576 | tf_op jit(solution)/shard_map/all_to_all | solution.py:189
  69.6 0.4 convolution_bitcast_fusion.3
  70.1 0.8 copy.66
  70.9 13.1 %all-to-all-done.1 = f32[16,1,1,4,2,8,128]{6,5,4,3,2,1,0:T(8,128)S(1)} async-done(((f32[16,1,1,4,2,8,128]{6,5,4,3,2,1,0:T(8,128)}), f32[16,1,1,4,2,8,128]{6,5,4,3,2,1,0:T(8,128)S(1)}, u32[]{:S(2)}, u32[]{:S(2)}) %all-to-all-start.1) | async-done | bytes 524320 | tf_op jit(solution)/shard_map/all_to_all | solution.py:189
  84.0 3.9 %all-to-all-start.5 = ((f32[16,1,1,4,2,8,128]{6,5,4,3,2,1,0:T(8,128)}), f32[16,1,1,4,2,8,128]{6,5,4,3,2,1,0:T(8,128)S(1)}, u32[]{:S(2)}, u32[]{:S(2)}) async-start(f32[16,1,1,4,2,8,128]{6,5,4,3,2,1,0:T(8,128)} %bitcast.117), calls=%async_computation.5 | async-start | bytes 1048576 | tf_op jit(solution)/shard_map/all_to_all | solution.py:189
  87.9 0.0 all-reduce.3.cloned.1.call-start
  88.0 0.3 copy.30
  88.2 1.6 fusion.20
  89.8 14.3 %shard_map.175 = (f32[2048,128]{1,0:T(8,128)}, bf16[2048,1024]{1,0:T(8,128)(2,1)}, bf16[2048,1024]{1,0:T(8,128)(2,1)}, bf16[2048,1024]{1,0:T(8,128)(2,1)}, bf16[2048,1024]{1,0:T(8,128)(2,1)}) custom-call(f32[2048,128]{1,0:T(8,128)} %bitcast.131, bf16[128,1024]{1,0:T(8,128)(2,1)} %refs_6_.3, bf16[1024,1024]{1,0:T(8,128)(2,1)} %refs_7_.3, ...), custom_call_target="tpu_custom_call" | custom-call | flops 5368709120 | bytes 16777216 | tf_op jit(solution)/shard_map/pallas_call | solution.py:83
  104.1 0.0 all-to-all-done.5
  104.1 0.3 copy.38
  104.4 1.5 fusion.21
  105.9 18.3 %shard_map.176 = (f32[128,1024]{1,0:T(8,128)}, f32[1024,1024]{1,0:T(8,128)}, f32[1024,128]{1,0:T(8,128)}, f32[2048,128]{1,0:T(8,128)}) custom-call(f32[2048,128]{1,0:T(8,128)} %bitcast.135, f32[2048,128]{1,0:T(8,128)} %bitcast.132, bf16[2048,1024]{1,0:T(8,128)(2,1)} %get-tuple-element.23.refs_2_, bf16[2048,1024]{1,0:T(8,128)(2,1)} %get-tuple-element.24.refs_3_, ...), custom_call_target="tpu_custom_call" | custom-call | flops 10737418240 | bytes 16777216 | tf_op jit(solution)/shard_map/pallas_call | solution.py:147
  124.2 1.6 convolution_bitcast_fusion.2
  125.9 20.5 %all_to_all.40 = f32[16,1,8,8,128]{4,2,3,1,0:T(8,128)S(1)} all-to-all(f32[16,1,8,8,128]{4,2,3,1,0:T(8,128)S(1)} %convolution_bitcast_fusion.2), channel_id=1, replica_groups=mesh['lat'=16,'dp'=2] {'lat'}, dimensions={0} | all-to-all | bytes 1048576 | tf_op jit(solution)/shard_map/all_to_all | solution.py:181
  146.4 0.4 convolution_bitcast_fusion.1
  146.9 17.4 %all_to_all.41 = f32[16,1,1,4,2,8,128]{6,5,4,3,2,1,0:T(8,128)S(1)} all-to-all(f32[16,1,1,4,2,8,128]{6,5,4,3,2,1,0:T(8,128)S(1)} %bitcast.128), channel_id=1, replica_groups=mesh['lat'=16,'dp'=2] {'lat'}, dimensions={0} | all-to-all | bytes 1048576 | tf_op jit(solution)/shard_map/all_to_all | solution.py:189
  164.4 0.3 copy.42
  164.6 1.5 fusion.22
  166.2 19.0 %shard_map.177 = (f32[128,1024]{1,0:T(8,128)}, f32[1024,1024]{1,0:T(8,128)}, f32[1024,128]{1,0:T(8,128)}) custom-call(f32[2048,128]{1,0:T(8,128)} %bitcast.133, f32[2048,128]{1,0:T(8,128)} %bitcast.138, bf16[2048,1024]{1,0:T(8,128)(2,1)} %get-tuple-element.28.refs_2_, bf16[2048,1024]{1,0:T(8,128)(2,1)} %get-tuple-element.29.refs_3_, ...), custom_call_target="tpu_custom_call" | custom-call | flops 10737418240 | bytes 16777216 | tf_op jit(solution)/shard_map/pallas_call | solution.py:147
  185.2 0.0 all-reduce.3.cloned.1.call-update
  185.2 1.2 copy-done.2
  186.4 0.4 convolution_bitcast_fusion.6
  186.9 25.9 %all_to_all.42 = f32[16,1,8,8,128]{4,2,3,1,0:T(8,128)S(1)} all-to-all(f32[16,1,8,8,128]{4,2,3,1,0:T(8,128)S(1)} %convolution_bitcast_fusion.6), channel_id=1, replica_groups=mesh['lat'=16,'dp'=2] {'lat'}, dimensions={0} | all-to-all | bytes 1048576 | tf_op jit(solution)/shard_map/all_to_all | solution.py:181
  212.7 0.4 convolution_bitcast_fusion.5
  213.3 22.6 %all_to_all.43 = f32[16,1,1,4,2,8,128]{6,5,4,3,2,1,0:T(8,128)S(1)} all-to-all(f32[16,1,1,4,2,8,128]{6,5,4,3,2,1,0:T(8,128)S(1)} %bitcast.129), channel_id=1, replica_groups=mesh['lat'=16,'dp'=2] {'lat'}, dimensions={0} | all-to-all | bytes 1048576 | tf_op jit(solution)/shard_map/all_to_all | solution.py:189
  235.8 0.3 copy.34
  236.1 1.5 convolution_bitcast_fusion
  237.6 114.9 %all-reduce.3.cloned.1.call-done = (f32[128,1024]{1,0:T(8,128)}, f32[1024,1024]{1,0:T(8,128)}, f32[1024,128]{1,0:T(8,128)}) async-done(((f32[128,1024]{1,0:T(8,128)}, f32[1024,1024]{1,0:T(8,128)}, f32[1024,128]{1,0:T(8,128)}), (f32[128,1024]{1,0:T(8,128)}, f32[1024,1024]{1,0:T(8,128)}, f32[1024,128]{1,0:T(8,128)})) %all-reduce.3.cloned.1.call-update) | async-done | bytes 5242896 | tf_op jit(solution)/shard_map/psum | solution.py:213
  352.6 2.0 copy.72
  354.5 4.8 %copy.73 = f32[1024,1024]{1,0:T(8,128)} copy(f32[1024,1024]{1,0:T(8,128)} %get-tuple-element.43) | data formatting | bytes 8388608
  359.4 0.8 copy.74
  (13 shorter events, 0.1 us)
Async XLA Ops:
  7.2 25.1 %copy-start = (f32[1,8,256,128]{3,2,1,0:T(8,128)S(1)}, f32[1,8,256,128]{3,2,1,0:T(8,128)}, u32[]{:S(2)}) copy-start(f32[1,8,256,128]{3,2,1,0:T(8,128)} %param.16) | copy-start | bytes 3145732
  7.2 14.3 %copy-start.5 = (f32[16,8,256,1]{2,1,3,0:T(8,128)S(1)}, f32[16,8,256,1]{2,1,3,0:T(8,128)}, u32[]{:S(2)}) copy-start(f32[16,8,256,1]{2,1,3,0:T(8,128)} %constant.31) | copy-start | bytes 393220
  7.2 25.1 %copy-start.7 = (f32[16,8,256,1]{2,1,3,0:T(8,128)S(1)}, f32[16,8,256,1]{2,1,3,0:T(8,128)}, u32[]{:S(2)}) copy-start(f32[16,8,256,1]{2,1,3,0:T(8,128)} %constant.33) | copy-start | bytes 393220
  21.5 31.5 %copy-start.8 = (f32[128]{0:T(128)S(1)}, f32[128]{0:T(128)}, u32[]{:S(2)}) copy-start(f32[128]{0:T(128)} %constant.21.clone) | copy-start | bytes 1540
  23.9 23.4 %all-to-all-start = ((f32[16,1,8,8,128]{4,2,3,1,0:T(8,128)}), f32[16,1,8,8,128]{4,2,3,1,0:T(8,128)S(1)}, u32[]{:S(2)}, u32[]{:S(2)}) async-start(f32[16,1,8,8,128]{4,2,3,1,0:T(8,128)} %convolution_bitcast_fusion.8), calls=%async_computation | async-start | bytes 1048576 | tf_op jit(solution)/shard_map/all_to_all | solution.py:181
  47.4 18.4 %all-to-all-start.4 = ((f32[16,1,8,8,128]{4,2,3,1,0:T(8,128)}), f32[16,1,8,8,128]{4,2,3,1,0:T(8,128)S(1)}, u32[]{:S(2)}, u32[]{:S(2)}) async-start(f32[16,1,8,8,128]{4,2,3,1,0:T(8,128)} %convolution_bitcast_fusion.4), calls=%async_computation.4 | async-start | bytes 1048576 | tf_op jit(solution)/shard_map/all_to_all | solution.py:181
  51.3 36.9 %copy-start.4 = (f32[256,128,1]{1,0,2:T(8,128)S(1)}, f32[256,128,1]{1,0,2:T(8,128)}, u32[]{:S(2)}) copy-start(f32[256,128,1]{1,0,2:T(8,128)} %constant.30) | copy-start | bytes 393220
  65.7 18.3 %all-to-all-start.1 = ((f32[16,1,1,4,2,8,128]{6,5,4,3,2,1,0:T(8,128)}), f32[16,1,1,4,2,8,128]{6,5,4,3,2,1,0:T(8,128)S(1)}, u32[]{:S(2)}, u32[]{:S(2)}) async-start(f32[16,1,1,4,2,8,128]{6,5,4,3,2,1,0:T(8,128)} %bitcast.119), calls=%async_computation.1 | async-start | bytes 1048576 | tf_op jit(solution)/shard_map/all_to_all | solution.py:189
  84.0 20.0 %all-to-all-start.5 = ((f32[16,1,1,4,2,8,128]{6,5,4,3,2,1,0:T(8,128)}), f32[16,1,1,4,2,8,128]{6,5,4,3,2,1,0:T(8,128)S(1)}, u32[]{:S(2)}, u32[]{:S(2)}) async-start(f32[16,1,1,4,2,8,128]{6,5,4,3,2,1,0:T(8,128)} %bitcast.117), calls=%async_computation.5 | async-start | bytes 1048576 | tf_op jit(solution)/shard_map/all_to_all | solution.py:189
  87.9 264.7 %all-reduce.3.cloned.1.call-start = ((), (), s32[]{:S(2)}) async-start(), calls=%async_computation.8 | async-start | bytes 10485760 | tf_op jit(solution)/shard_map/psum | solution.py:213
  89.8 14.6 %copy-start.6 = (f32[256,128,1]{1,0,2:T(8,128)S(1)}, f32[256,128,1]{1,0,2:T(8,128)}, u32[]{:S(2)}) copy-start(f32[256,128,1]{1,0,2:T(8,128)} %constant.32) | copy-start | bytes 393220
  185.2 1.2 copy-start.2
  352.6 7.6 %copy-start.1 = (f32[1,8,256,128]{3,2,1,0:T(8,128)S(1)}, f32[1,8,256,128]{3,2,1,0:T(8,128)}, u32[]{:S(2)}) copy-start(f32[1,8,256,128]{3,2,1,0:T(8,128)} %param.16) | copy-start | bytes 3145732
  354.5 4.8 %copy-start.3 = (f32[1024,128]{1,0:T(8,128)S(1)}, f32[1024,128]{1,0:T(8,128)}, u32[]{:S(2)}) copy-start(f32[1024,128]{1,0:T(8,128)} %get-tuple-element.44) | copy-start | bytes 1572868
Sparse Core Ops, SparseCore 0:
  185.4 167.1 all-reduce.2
